TPU v7x, 32 devices: a whole 2x2x4 slice. The times are simulated.
32 devices in a mesh: dp: 8 (over y, x, core), tm: 4 (over z).
Axes of the slice: x: 2, y: 2, z: 4, core: 2. Of those that a mesh axis runs over, the one named last changes fastest.
Arguments:
- tokens: bfloat16 [8, 4, 256, 1024], P('dp', 'tm'), may hold values from -6 to 6
- gain: bfloat16 [1024], replicated, may hold values from 0.25 to 1.75
- w_qkv: bfloat16 [1024, 3072], P('dp'), may hold values from -0.1875 to 0.1875
- w_out: bfloat16 [1024, 1024], P('dp'), may hold values from -0.1875 to 0.1875
- w_pair: float32 [2, 1024, 32], replicated, may hold values from -3 to 3
- codebook: float32 [8, 32], replicated, may hold values from -5 to 5
- codes: int32 [8, 4, 1], P('dp', 'tm'), may hold values from 0 to 7
Outputs:
- grad_tokens: bfloat16 [8, 4, 256, 1024], P('dp', 'tm')
- grad_pair: float32 [2, 1024, 32], replicated
- codebook_step: float32 [8, 32], replicated
Inputs may be any that keep to these rules, and one draw needn't show every extreme that they name: Every one of the 8 codes is assigned to some clip frame.
All inputs are finite; a program needn't handle non-finite values.
Results may differ from a plain program's by a relative error of at most 0.014.
Values may be sent and summed in bfloat16 or wider, within the bound.
A program may use at most 64 MiB of HBM per device.

v0:
```python
import jax
import jax.numpy as jnp
from jax import lax
from jax.sharding import PartitionSpec as P

D = 1024
HEAD_DIM = 64
CODES = 8
PATCHES = 256
EPS = 1e-06
BETA = 0.25


def passed_along(value, axis, by):
    count = lax.axis_size(axis)
    pairs = [(i, i + by) for i in range(count) if 0 <= i + by < count]
    return lax.ppermute(value, axis, pairs)


def normalize(xf, gain):
    scale = lax.rsqrt(jnp.mean(xf * xf, axis=-1, keepdims=True) + EPS)
    return (xf * scale * gain.astype(jnp.float32)).astype(jnp.bfloat16)


def project(normed, weight):
    shape = normed.shape
    flat = jnp.dot(normed.reshape(-1, shape[-1]), weight, preferred_element_type=jnp.float32)
    return flat.astype(jnp.bfloat16).reshape(shape[:-1] + (3, shape[-1]))


def attend(qkv):
    clips, frames, patches, _, width = qkv.shape
    local_heads = width // HEAD_DIM
    parts = qkv.reshape(clips, frames, patches, 3, local_heads, HEAD_DIM)
    query = parts[:, :, :, 0].astype(jnp.float32)
    keys = parts[:, :, :, 1].astype(jnp.float32)
    values = parts[:, :, :, 2].astype(jnp.float32)
    scores = jnp.einsum("cfphd,cgphd->cphfg", query, keys) * HEAD_DIM ** (-0.5)
    causal = jnp.arange(frames)[:, None] >= jnp.arange(frames)[None, :]
    scores = jnp.where(causal, scores, -1e30)
    weights = jax.nn.softmax(scores, axis=-1).astype(jnp.bfloat16)
    mixed = jnp.einsum("cphfg,cgphd->cfphd", weights.astype(jnp.float32), values)
    return mixed.reshape(clips, frames, patches, width).astype(jnp.bfloat16)


def output(xf, attended, weight):
    shape = xf.shape
    moved = jnp.dot(attended.reshape(-1, shape[-1]), weight, preferred_element_type=jnp.float32)
    return jnp.mean(xf + moved.reshape(shape), axis=2)


def local(tokens, gain, w_qkv, w_out, w_pair, codebook, codes):
    xf = tokens.astype(jnp.float32)
    groups = lax.axis_size("tm")
    full_out = w_out
    full_qkv, full_out = (
        lax.all_gather(w_qkv, "dp", axis=0, tiled=True),
        lax.all_gather(w_out, "dp", axis=0, tiled=True),
    )
    normed, norm_back = jax.vjp(lambda value: normalize(value, gain), xf)
    regrouped = lax.all_to_all(normed, "tm", split_axis=2, concat_axis=1, tiled=True)
    qkv, qkv_back = jax.vjp(lambda value: project(value, full_qkv), regrouped)
    attended, attend_back = jax.vjp(attend, qkv)
    lifted = attended[:, :, None]
    returned = lax.all_to_all(lifted, "tm", split_axis=1, concat_axis=2, tiled=True)
    clips_here, frames_here = (returned.shape[0], returned.shape[1])
    local_out = returned.reshape(clips_here, frames_here, -1, D)
    pooled, out_back = jax.vjp(lambda first, second: output(first, second, full_out), xf, local_out)
    following = passed_along(pooled, "tm", -1)
    flat_now = pooled.reshape(-1, D)
    flat_next = following.reshape(-1, D)
    highest = lax.Precision.HIGHEST
    action = jnp.dot(flat_now, w_pair[0], precision=highest) + jnp.dot(
        flat_next, w_pair[1], precision=highest
    )
    onehot = (codes.reshape(-1)[:, None] == jnp.arange(CODES)[None, :]).astype(jnp.float32)
    quantized = jnp.dot(onehot, codebook, precision=highest)
    diff = action - quantized
    d_action = 2.0 * BETA * diff
    d_quant = -2.0 * diff
    pair_part = jnp.stack(
        [
            jnp.dot(flat_now.T, d_action, precision=highest),
            jnp.dot(flat_next.T, d_action, precision=highest),
        ]
    )
    code_part = jnp.dot(onehot.T, d_quant, precision=highest)
    count_part = jnp.sum(onehot, axis=0)
    grad_pair, code_total, count = lax.psum((pair_part, code_part, count_part), ("dp", "tm"))
    codebook_step = code_total / count[:, None]
    d_own = jnp.dot(d_action, w_pair[0].T, precision=highest).reshape(pooled.shape)
    d_next = jnp.dot(d_action, w_pair[1].T, precision=highest).reshape(pooled.shape)
    carried = passed_along(d_next, "tm", 1)
    d_pooled = (d_own + carried) * PATCHES
    d_resid, d_local = out_back(d_pooled)
    clips_here, frames_here, rows_here = (d_local.shape[0], d_local.shape[1], d_local.shape[2])
    spread = d_local.reshape(clips_here, frames_here, groups, rows_here // groups, D)
    gathered_back = lax.all_to_all(spread, "tm", split_axis=2, concat_axis=1, tiled=True)
    d_attended = gathered_back.reshape(attended.shape)
    (d_qkv,) = attend_back(d_attended)
    (d_regrouped,) = qkv_back(d_qkv)
    d_normed = lax.all_to_all(d_regrouped, "tm", split_axis=1, concat_axis=2, tiled=True)
    (d_through,) = norm_back(d_normed)
    grad_tokens = (d_resid + d_through).astype(jnp.bfloat16)
    return (grad_tokens, grad_pair, codebook_step)


def solution(mesh):
    placed = (
        P("dp", "tm", None, None),
        P(),
        P("dp", None),
        P("dp", None),
        P(),
        P(),
        P("dp", "tm", None),
    )
    return jax.shard_map(
        local,
        mesh=mesh,
        in_specs=placed,
        out_specs=(P("dp", "tm", None, None), P(), P()),
        check_vma=False,
    )
```

profile of v0, /device:TPU:0, one launch (start us, length us, event | category | flops | bytes accessed | tf_op | source)
XLA Modules:
  0.0 300.7 jit_solution(16761562726995000602)
XLA Ops:
  7.2 0.7 all-gather.3.cloned.1.call-update
  7.9 0.7 convert_element_type.110
  8.6 1.2 fusion.15
  9.8 1.2 fusion.17
  11.1 0.8 copy.83
  12.4 3.9 %reduce.9 = bf16[256,1024]{1,0:T(8,128)(2,1)S(1)} reduce(bf16[256,1,1,1024]{3,2,1,0:T(2,128)(2,1)S(1)} %bitcast.152, bf16[]{:T(256)} %broadcast.182), dimensions={1,2}, to_apply=%bitcast.147.reduce_sub_computation | reduce | bytes 1048578
  16.4 1.2 reshape.366
  17.5 6.3 %all-to-all-start = ((bf16[4,2,32768]{2,1,0:T(2,128)(2,1)}), bf16[4,2,32768]{2,1,0:T(2,128)(2,1)S(1)}, u32[]{:S(2)}, u32[]{:S(2)}) async-start(bf16[4,2,32768]{2,1,0:T(2,128)(2,1)} %reshape.366), calls=%async_computation | async-start | bytes 1048576 | tf_op jit(solution)/shard_map/all_to_all | solution.py:61
  23.9 0.7 all-gather.5.cloned.1.call-update
  24.6 13.7 %all-to-all-done = bf16[4,2,32768]{2,1,0:T(2,128)(2,1)S(1)} async-done(((bf16[4,2,32768]{2,1,0:T(2,128)(2,1)}), bf16[4,2,32768]{2,1,0:T(2,128)(2,1)S(1)}, u32[]{:S(2)}, u32[]{:S(2)}) %all-to-all-start) | async-done | bytes 524320 | tf_op jit(solution)/shard_map/all_to_all | solution.py:61
  38.4 0.5 reshape.367
  38.9 19.1 %all-gather.3.cloned.1.call-done = bf16[1024,3072]{1,0:T(8,128)(2,1)} async-done(((bf16[128,3072]{1,0:T(8,128)(2,1)}), bf16[1024,3072]{1,0:T(8,128)(2,1)}) %all-gather.3.cloned.1.call-update) | async-done | bytes 6291472 | tf_op jit(solution)/shard_map/all_gather | solution.py:57
  58.0 5.8 %convolution_convert_fusion = bf16[256,3072]{1,0:T(8,128)(2,1)} fusion(bf16[1024,3072]{1,0:T(8,128)(2,1)} %all-gather.3.cloned.1.call-done, bf16[1,1,256,1024]{3,1,0,2:T(2,128)(2,1)S(1)} %bitcast.154), kind=kOutput, calls=%fused_computation.1 | convolution fusion | flops 1611399168 | bytes 8388608 | tf_op jit(solution)/shard_map/jvp()/dot_general | solution.py:27
  63.8 3.7 %reshape.339 = bf16[1,4,64,3,16,64]{5,4,3,2,1,0:T(8,128)(2,1)S(1)} reshape(bf16[256,3072]{1,0:T(8,128)(2,1)} %convolution_convert_fusion) | data formatting | bytes 3145728 | tf_op jit(solution)/shard_map/jvp()/reshape;jvp()/reshape | solution.py:34
  67.5 1.9 fusion.43
  69.4 5.3 %fusion.44 = (f32[64,16,4]{2,1,0:T(8,128)S(1)}, f32[64,16,4,4]{2,3,1,0:T(4,128)S(1)}) fusion(pred[4,4]{0,1:T(4,128)(4,1)S(1)} %iota_compare_fusion, bf16[1,4,64,1,16,64]{5,4,3,2,1,0:T(8,128)(2,1)} %get-tuple-element.6, bf16[1,4,64,1,16,64]{5,4,3,2,1,0:T(8,128)(2,1)} %get-tuple-element.7), kind=kOutput, calls=%fused_computation.88 | convolution fusion | flops 2162691 | bytes 1130512 | tf_op jit(solution)/shard_map/jvp()/sub | solution.py:41
  74.7 0.6 divide_convert_fusion
  75.4 1.0 copy-done.3
  76.4 1.6 fusion.5
  78.0 1.2 copy.40
  79.2 2.6 convert_element_type.117
  81.8 4.6 %all-to-all-start.1 = ((bf16[1,4,1,64,1024]{4,3,2,0,1:T(8,128)(2,1)}), bf16[1,4,1,64,1024]{4,3,2,0,1:T(8,128)(2,1)}, u32[]{:S(2)}, u32[]{:S(2)}) async-start(bf16[1,4,1,64,1024]{4,3,2,0,1:T(8,128)(2,1)} %bitcast.153), calls=%async_computation.1 | async-start | bytes 1048576 | tf_op jit(solution)/shard_map/all_to_all | solution.py:65
  87.7 13.7 %all-to-all-done.1 = bf16[1,4,1,64,1024]{4,3,2,0,1:T(8,128)(2,1)} async-done(((bf16[1,4,1,64,1024]{4,3,2,0,1:T(8,128)(2,1)}), bf16[1,4,1,64,1024]{4,3,2,0,1:T(8,128)(2,1)}, u32[]{:S(2)}, u32[]{:S(2)}) %all-to-all-start.1) | async-done | bytes 524320 | tf_op jit(solution)/shard_map/all_to_all | solution.py:65
  101.4 2.6 fusion.9
  104.1 1.3 collective-permute-start
  105.6 4.0 %collective-permute-done = f32[1,1,1024]{2,1,0:T(1,128)S(1)} collective-permute-done((f32[1,1,1024]{2,1,0:T(1,128)S(1)}, f32[1,1,1024]{2,1,0:T(1,128)S(1)}, u32[]{:S(2)}, u32[]{:S(2)}) %collective-permute-start) | collective-permute-done | bytes 4128 | tf_op jit(solution)/shard_map/ppermute | solution.py:17
  110.0 1.7 collective-permute-start.1
  111.6 1.3 collective-permute-done.1
  113.2 1.6 convolution_convert_fusion.7
  114.7 3.7 %all-to-all-start.2 = ((bf16[1,1,4,64,1024]{4,3,1,0,2:T(8,128)(2,1)}), bf16[1,1,4,64,1024]{4,3,1,0,2:T(8,128)(2,1)S(1)}, u32[]{:S(2)}, u32[]{:S(2)}) async-start(bf16[1,1,4,64,1024]{4,3,1,0,2:T(8,128)(2,1)} %bitcast.155), calls=%async_computation.2 | async-start | bytes 1048576 | tf_op jit(solution)/shard_map/all_to_all | solution.py:98
  118.4 0.9 multiply_divide_fusion
  119.3 11.2 %all-to-all-done.2 = bf16[1,1,4,64,1024]{4,3,1,0,2:T(8,128)(2,1)S(1)} async-done(((bf16[1,1,4,64,1024]{4,3,1,0,2:T(8,128)(2,1)}), bf16[1,1,4,64,1024]{4,3,1,0,2:T(8,128)(2,1)S(1)}, u32[]{:S(2)}, u32[]{:S(2)}) %all-to-all-start.2) | async-done | bytes 524320 | tf_op jit(solution)/shard_map/all_to_all | solution.py:98
  130.5 1.7 reshape.349
  132.2 2.9 fusion.6
  135.1 2.7 fusion.4
  137.9 1.4 select_multiply_fusion
  139.3 1.2 fusion.7
  140.6 1.6 fusion.8
  142.2 3.1 %pad_add_fusion = bf16[1,4,64,3,16,64]{5,1,4,2,3,0:T(4,128)(2,1)S(1)} fusion(bf16[1,4,64,1,16,64]{5,1,4,2,3,0:T(4,128)(2,1)S(1)} %fusion.8, bf16[1,4,64,1,16,64]{5,1,4,2,3,0:T(4,128)(2,1)S(1)} %fusion.7, bf16[1,4,64,1,16,64]{5,1,4,2,3,0:T(4,128)(2,1)S(1)} %fusion.6), kind=kLoop, calls=%fused_computation.2 | loop fusion | flops 1572864 | bytes 3145728 | tf_op jit(solution)/shard_map/transpose(jvp())/add_any | solution.py:35
  145.8 3.2 %reshape.351 = bf16[256,3072]{1,0:T(8,128)(2,1)} reshape(bf16[1,4,64,3,16,64]{5,4,3,2,1,0:T(8,128)(2,1)S(1)} %copy.45) | data formatting | bytes 3145728 | tf_op jit(solution)/shard_map/transpose(jvp())/reshape;transpose(jvp())/reshape | solution.py:28
  149.0 5.9 %convolution_convert_fusion.6 = bf16[256,1024]{1,0:T(8,128)(2,1)} fusion(bf16[256,3072]{1,0:T(8,128)(2,1)} %reshape.351, bf16[1024,3072]{1,0:T(8,128)(2,1)} %all-gather.3.cloned.1.call-done), kind=kOutput, calls=%fused_computation.29 | convolution fusion | flops 1610874880 | bytes 8388608 | tf_op jit(solution)/shard_map/transpose(jvp())/dot_general | solution.py:27
  154.9 3.6 %all-to-all-start.3 = ((bf16[1,4,64,1024]{3,2,0,1:T(8,128)(2,1)}), bf16[1,4,64,1024]{3,2,0,1:T(8,128)(2,1)S(1)}, u32[]{:S(2)}, u32[]{:S(2)}) async-start(bf16[1,4,64,1024]{3,2,0,1:T(8,128)(2,1)} %bitcast.41), calls=%async_computation.3 | async-start | bytes 1048576 | tf_op jit(solution)/shard_map/all_to_all | solution.py:102
  158.6 0.7 pad_maximum_fusion
  159.5 39.8 %all-reduce.3 = (f32[8,32]{1,0:T(8,128)S(1)}, f32[8]{0:T(128)S(1)}) all-reduce(f32[8,32]{1,0:T(8,128)S(1)} %broadcast_multiply_fusion, f32[8]{0:T(128)S(1)} %compare_convert_fusion), channel_id=1, replica_groups=mesh['dp'=8,'tm'=4] {'dp','tm'}, use_global_device_ids=true, to_apply=%region_7.8 | all-reduce | flops 264 | bytes 2112 | tf_op jit(solution)/shard_map/psum | solution.py:89
  199.3 0.7 broadcast_divide_fusion
  200.2 1.1 fusion.14
  201.4 91.1 %all-reduce.6.cloned.1.call-done = f32[2,1024,32]{1,2,0:T(8,128)} async-done(((f32[2,1024,32]{1,2,0:T(8,128)}), f32[2,1024,32]{1,2,0:T(8,128)}) %all-reduce.6.cloned.1.call-update) | async-done | bytes 262160 | tf_op jit(solution)/shard_map/psum | solution.py:89
  292.5 1.7 copy.86
  (45 shorter events, 2.9 us)
Async XLA Ops:
  7.2 80.0 %copy-start = (f32[8,32]{1,0:T(8,128)S(1)}, f32[8,32]{1,0:T(8,128)}, u32[]{:S(2)}) copy-start(f32[8,32]{1,0:T(8,128)} %param.12) | copy-start | bytes 3076
  7.2 50.8 %all-gather.3.cloned.1.call-start = ((), (), s32[]{:S(2)}) async-start(), calls=%async_computation.4 | async-start | bytes 7077888 | tf_op jit(solution)/shard_map/all_gather | solution.py:57
  17.5 20.8 %all-to-all-start = ((bf16[4,2,32768]{2,1,0:T(2,128)(2,1)}), bf16[4,2,32768]{2,1,0:T(2,128)(2,1)S(1)}, u32[]{:S(2)}, u32[]{:S(2)}) async-start(bf16[4,2,32768]{2,1,0:T(2,128)(2,1)} %reshape.366), calls=%async_computation | async-start | bytes 1048576 | tf_op jit(solution)/shard_map/all_to_all | solution.py:61
  23.9 63.8 %all-gather.5.cloned.1.call-start = ((), (), s32[]{:S(2)}) async-start(), calls=%async_computation.5 | async-start | bytes 2359296 | tf_op jit(solution)/shard_map/all_gather | solution.py:58
  74.7 1.6 copy-start.8
  75.4 1.0 copy-start.3
  78.0 23.4 %copy-start.1 = (bf16[1,1,256,1024]{3,2,1,0:T(8,128)(2,1)S(1)}, bf16[1,1,256,1024]{3,2,1,0:T(8,128)(2,1)}, u32[]{:S(2)}) copy-start(bf16[1,1,256,1024]{3,2,1,0:T(8,128)(2,1)} %param.7) | copy-start | bytes 1572868
  81.8 19.6 %all-to-all-start.1 = ((bf16[1,4,1,64,1024]{4,3,2,0,1:T(8,128)(2,1)}), bf16[1,4,1,64,1024]{4,3,2,0,1:T(8,128)(2,1)}, u32[]{:S(2)}, u32[]{:S(2)}) async-start(bf16[1,4,1,64,1024]{4,3,2,0,1:T(8,128)(2,1)} %bitcast.153), calls=%async_computation.1 | async-start | bytes 1048576 | tf_op jit(solution)/shard_map/all_to_all | solution.py:65
  86.4 19.0 %copy-start.5 = (f32[2,1024,32]{1,2,0:T(8,128)S(1)}, f32[2,1024,32]{1,2,0:T(8,128)}, u32[]{:S(2)}) copy-start(f32[2,1024,32]{1,2,0:T(8,128)} %param.11) | copy-start | bytes 786436
  101.4 11.7 %copy-start.11 = (bf16[1024,1024]{1,0:T(8,128)(2,1)S(1)}, bf16[1024,1024]{1,0:T(8,128)(2,1)}, u32[]{:S(2)}) copy-start(bf16[1024,1024]{1,0:T(8,128)(2,1)} %all-gather.5.cloned.1.call-done) | copy-start | bytes 6291460
  104.1 5.5 %collective-permute-start = (f32[1,1,1024]{2,1,0:T(1,128)S(1)}, f32[1,1,1024]{2,1,0:T(1,128)S(1)}, u32[]{:S(2)}, u32[]{:S(2)}) collective-permute-start(f32[1,1,1024]{2,1,0:T(1,128)S(1)} %bitcast.156), channel_id=1, source_target_pairs={{1,0},{2,1},{3,2},{5,4},{6,5},{7,6},{9,8},{10,9},{11,10},{13,12},{... | collective-permute-start | bytes 12296 | tf_op jit(solution)/shard_map/ppermute | solution.py:17
  110.0 3.0 collective-permute-start.1
  114.7 15.8 %all-to-all-start.2 = ((bf16[1,1,4,64,1024]{4,3,1,0,2:T(8,128)(2,1)}), bf16[1,1,4,64,1024]{4,3,1,0,2:T(8,128)(2,1)S(1)}, u32[]{:S(2)}, u32[]{:S(2)}) async-start(bf16[1,1,4,64,1024]{4,3,1,0,2:T(8,128)(2,1)} %bitcast.155), calls=%async_computation.2 | async-start | bytes 1048576 | tf_op jit(solution)/shard_map/all_to_all | solution.py:98
  132.2 2.9 copy-start.4
  132.2 2.9 copy-start.9
  132.2 2.9 copy-start.10
  137.9 1.4 copy-start.7
  139.3 1.2 copy-start.6
  154.9 45.1 %copy-start.2 = (bf16[1,1,256,1024]{3,2,1,0:T(8,128)(2,1)S(1)}, bf16[1,1,256,1024]{3,2,1,0:T(8,128)(2,1)}, u32[]{:S(2)}) copy-start(bf16[1,1,256,1024]{3,2,1,0:T(8,128)(2,1)} %param.7) | copy-start | bytes 1572868
  154.9 45.1 %all-to-all-start.3 = ((bf16[1,4,64,1024]{3,2,0,1:T(8,128)(2,1)}), bf16[1,4,64,1024]{3,2,0,1:T(8,128)(2,1)S(1)}, u32[]{:S(2)}, u32[]{:S(2)}) async-start(bf16[1,4,64,1024]{3,2,0,1:T(8,128)(2,1)} %bitcast.41), calls=%async_computation.3 | async-start | bytes 1048576 | tf_op jit(solution)/shard_map/all_to_all | solution.py:102
  158.5 134.0 %all-reduce.6.cloned.1.call-start = ((), (), s32[]{:S(2)}) async-start(), calls=%async_computation.6 | async-start | bytes 524288 | tf_op jit(solution)/shard_map/psum | solution.py:89
Sparse Core Ops, SparseCore 0:
  9.9 48.1 all-gather.2
  59.9 27.7 all-gather.4
  165.4 127.0 all-reduce.5
where the time goes:
time: 301 us
  waiting for transfers between devices  156 us (52%)
  blocking collectives  39.8 us (13%)
  matrix products  32.2 us (11%)
  starting transfers between devices  21.3 us (7%)
  local copies, waits for them, and re-layouts  20.4 us (7%)
  other arithmetic  16.1 us (5%)
  between operations  14.8 us (5%)
    psum x1, waiting for transfers between devices, local(): lax.psum((pair_part, code_part, count_part), ('dp', 'tm'))  91.1 us
    psum x1, blocking collectives, local(): lax.psum((pair_part, code_part, count_part), ('dp', 'tm'))  39.8 us
    all_gather x1, waiting for transfers between devices, local(): lax.all_gather(w_qkv, 'dp', axis=0, tiled=True)  19.1 us
    all_to_all x1, waiting for transfers between devices, local(): lax.all_to_all(normed, 'tm', split_axis=2, concat_axis=1, tiled=True)  13.7 us
    all_to_all x1, waiting for transfers between devices, local(): lax.all_to_all(lifted, 'tm', split_axis=1, concat_axis=2, tiled=True)  13.7 us
    dot_general x2, matrix products, project(): jnp.dot(normed.reshape(-1, shape[-1]), weight, preferred_element_type=jnp...  11.7 us
    all_to_all x1, waiting for transfers between devices, local(): lax.all_to_all(spread, 'tm', split_axis=2, concat_axis=1, tiled=True)  11.2 us
    dot_general x3, matrix products, attend(): jnp.einsum('cphfg,cgphd->cfphd', weights.astype(jnp.float32), values)  7.25 us
  transfers between devices with their start and end apart: 9, of which 8 were waited for; matrix products, arithmetic and copies ran while one was open for 12% of the time, Pallas kernels for 0%

commit v1 on v0

--- a/solution.py
+++ b/solution.py
@@ -86,7 +86,9 @@
     )
     code_part = jnp.dot(onehot.T, d_quant, precision=highest)
     count_part = jnp.sum(onehot, axis=0)
-    grad_pair, code_total, count = lax.psum((pair_part, code_part, count_part), ("dp", "tm"))
+    grad_pair, code_total, count = lax.psum(
+        lax.psum((pair_part, code_part, count_part), "tm"), "dp"
+    )
     codebook_step = code_total / count[:, None]
     d_own = jnp.dot(d_action, w_pair[0].T, precision=highest).reshape(pooled.shape)
     d_next = jnp.dot(d_action, w_pair[1].T, precision=highest).reshape(pooled.shape)

time: 301 us -> 264 us (0.88)
  waiting for transfers between devices: 156 us -> 134 us
  blocking collectives: 39.8 us -> 25 us
    psum x1 -> x2, waiting for transfers between devices: 91.1 us -> 68.6 us  [the longest x1 55.3 us: local(): lax.psum(lax.psum((pair_part, code_part, count_part), 'tm'), 'dp')]
    psum x1 -> x2, blocking collectives: 39.8 us -> 25 us  [the longest x1 12.7 us: local(): lax.psum((pair_part, code_part, count_part), 'tm')]
  transfers between devices with their start and end apart: 9 -> 10, of which waited for: 8 -> 9; matrix products, arithmetic and copies ran while one was open for 12% -> 14% of each run, Pallas kernels for 0% -> 0%
where the time goes in v1:
time: 264 us; the launch traced here: 263 us
  waiting for transfers between devices  134 us (51%)
  matrix products  32.2 us (12%)
  blocking collectives  25 us (9%)
  starting transfers between devices  21.3 us (8%)
  local copies, waits for them, and re-layouts  20.4 us (8%)
  other arithmetic  16.1 us (6%)
  between operations  14.8 us (6%)
    psum x1, waiting for transfers between devices, local(): lax.psum(lax.psum((pair_part, code_part, count_part), 'tm'), 'dp')  55.3 us
    all_gather x1, waiting for transfers between devices, local(): lax.all_gather(w_qkv, 'dp', axis=0, tiled=True)  19.1 us
    all_to_all x1, waiting for transfers between devices, local(): lax.all_to_all(normed, 'tm', split_axis=2, concat_axis=1, tiled=True)  13.7 us
    all_to_all x1, waiting for transfers between devices, local(): lax.all_to_all(lifted, 'tm', split_axis=1, concat_axis=2, tiled=True)  13.7 us
    psum x1, waiting for transfers between devices, local(): lax.psum((pair_part, code_part, count_part), 'tm')  13.3 us
    psum x1, blocking collectives, local(): lax.psum((pair_part, code_part, count_part), 'tm')  12.7 us
    psum x1, blocking collectives, local(): lax.psum(lax.psum((pair_part, code_part, count_part), 'tm'), 'dp')  12.3 us
    dot_general x2, matrix products, project(): jnp.dot(normed.reshape(-1, shape[-1]), weight, preferred_element_type=jnp...  11.7 us
  transfers between devices with their start and end apart: 10, of which 9 were waited for; matrix products, arithmetic and copies ran while one was open for 14% of the time, Pallas kernels for 0%

profile of v1, /device:TPU:0, one launch (start us, length us, event | category | flops | bytes accessed | tf_op | source)
XLA Modules:
  0.0 263.4 jit_solution(7530957886521481196)
XLA Ops:
  7.2 0.7 all-gather.3.cloned.1.call-update
  7.9 0.7 convert_element_type.110
  8.6 1.2 fusion.15
  9.8 1.2 fusion.17
  11.1 0.8 copy.83
  12.4 3.9 %reduce.9 = bf16[256,1024]{1,0:T(8,128)(2,1)S(1)} reduce(bf16[256,1,1,1024]{3,2,1,0:T(2,128)(2,1)S(1)} %bitcast.152, bf16[]{:T(256)} %broadcast.182), dimensions={1,2}, to_apply=%bitcast.147.reduce_sub_computation | reduce | bytes 1048578
  16.4 1.2 reshape.366
  17.5 6.3 %all-to-all-start = ((bf16[4,2,32768]{2,1,0:T(2,128)(2,1)}), bf16[4,2,32768]{2,1,0:T(2,128)(2,1)S(1)}, u32[]{:S(2)}, u32[]{:S(2)}) async-start(bf16[4,2,32768]{2,1,0:T(2,128)(2,1)} %reshape.366), calls=%async_computation | async-start | bytes 1048576 | tf_op jit(solution)/shard_map/all_to_all | solution.py:61
  23.9 0.7 all-gather.5.cloned.1.call-update
  24.6 13.7 %all-to-all-done = bf16[4,2,32768]{2,1,0:T(2,128)(2,1)S(1)} async-done(((bf16[4,2,32768]{2,1,0:T(2,128)(2,1)}), bf16[4,2,32768]{2,1,0:T(2,128)(2,1)S(1)}, u32[]{:S(2)}, u32[]{:S(2)}) %all-to-all-start) | async-done | bytes 524320 | tf_op jit(solution)/shard_map/all_to_all | solution.py:61
  38.9 19.1 %all-gather.3.cloned.1.call-done = bf16[1024,3072]{1,0:T(8,128)(2,1)} async-done(((bf16[128,3072]{1,0:T(8,128)(2,1)}), bf16[1024,3072]{1,0:T(8,128)(2,1)}) %all-gather.3.cloned.1.call-update) | async-done | bytes 6291472 | tf_op jit(solution)/shard_map/all_gather | solution.py:57
  58.0 5.8 %convolution_convert_fusion = bf16[256,3072]{1,0:T(8,128)(2,1)} fusion(bf16[1024,3072]{1,0:T(8,128)(2,1)} %all-gather.3.cloned.1.call-done, bf16[1,1,256,1024]{3,1,0,2:T(2,128)(2,1)S(1)} %bitcast.154), kind=kOutput, calls=%fused_computation.1 | convolution fusion | flops 1611399168 | bytes 8388608 | tf_op jit(solution)/shard_map/jvp()/dot_general | solution.py:27
  63.8 3.7 %reshape.339 = bf16[1,4,64,3,16,64]{5,4,3,2,1,0:T(8,128)(2,1)S(1)} reshape(bf16[256,3072]{1,0:T(8,128)(2,1)} %convolution_convert_fusion) | data formatting | bytes 3145728 | tf_op jit(solution)/shard_map/jvp()/reshape;jvp()/reshape | solution.py:34
  67.5 1.9 fusion.43
  69.4 5.3 %fusion.44 = (f32[64,16,4]{2,1,0:T(8,128)S(1)}, f32[64,16,4,4]{2,3,1,0:T(4,128)S(1)}) fusion(pred[4,4]{0,1:T(4,128)(4,1)S(1)} %iota_compare_fusion, bf16[1,4,64,1,16,64]{5,4,3,2,1,0:T(8,128)(2,1)} %get-tuple-element.8, bf16[1,4,64,1,16,64]{5,4,3,2,1,0:T(8,128)(2,1)} %get-tuple-element.9), kind=kOutput, calls=%fused_computation.88 | convolution fusion | flops 2162691 | bytes 1130512 | tf_op jit(solution)/shard_map/jvp()/sub | solution.py:41
  75.4 1.0 copy-done.3
  76.4 1.6 fusion.5
  78.0 1.2 copy.40
  79.2 2.6 convert_element_type.117
  81.8 4.6 %all-to-all-start.1 = ((bf16[1,4,1,64,1024]{4,3,2,0,1:T(8,128)(2,1)}), bf16[1,4,1,64,1024]{4,3,2,0,1:T(8,128)(2,1)}, u32[]{:S(2)}, u32[]{:S(2)}) async-start(bf16[1,4,1,64,1024]{4,3,2,0,1:T(8,128)(2,1)} %bitcast.153), calls=%async_computation.1 | async-start | bytes 1048576 | tf_op jit(solution)/shard_map/all_to_all | solution.py:65
  87.7 13.7 %all-to-all-done.1 = bf16[1,4,1,64,1024]{4,3,2,0,1:T(8,128)(2,1)} async-done(((bf16[1,4,1,64,1024]{4,3,2,0,1:T(8,128)(2,1)}), bf16[1,4,1,64,1024]{4,3,2,0,1:T(8,128)(2,1)}, u32[]{:S(2)}, u32[]{:S(2)}) %all-to-all-start.1) | async-done | bytes 524320 | tf_op jit(solution)/shard_map/all_to_all | solution.py:65
  101.4 2.6 fusion.9
  104.1 1.3 collective-permute-start
  105.6 4.0 %collective-permute-done = f32[1,1,1024]{2,1,0:T(1,128)S(1)} collective-permute-done((f32[1,1,1024]{2,1,0:T(1,128)S(1)}, f32[1,1,1024]{2,1,0:T(1,128)S(1)}, u32[]{:S(2)}, u32[]{:S(2)}) %collective-permute-start) | collective-permute-done | bytes 4128 | tf_op jit(solution)/shard_map/ppermute | solution.py:17
  110.0 1.7 collective-permute-start.1
  111.6 1.3 collective-permute-done.1
  113.1 1.6 convolution_convert_fusion.7
  114.7 3.7 %all-to-all-start.2 = ((bf16[1,1,4,64,1024]{4,3,1,0,2:T(8,128)(2,1)}), bf16[1,1,4,64,1024]{4,3,1,0,2:T(8,128)(2,1)S(1)}, u32[]{:S(2)}, u32[]{:S(2)}) async-start(bf16[1,1,4,64,1024]{4,3,1,0,2:T(8,128)(2,1)} %bitcast.155), calls=%async_computation.2 | async-start | bytes 1048576 | tf_op jit(solution)/shard_map/all_to_all | solution.py:100
  118.4 0.9 multiply_divide_fusion
  119.3 11.2 %all-to-all-done.2 = bf16[1,1,4,64,1024]{4,3,1,0,2:T(8,128)(2,1)S(1)} async-done(((bf16[1,1,4,64,1024]{4,3,1,0,2:T(8,128)(2,1)}), bf16[1,1,4,64,1024]{4,3,1,0,2:T(8,128)(2,1)S(1)}, u32[]{:S(2)}, u32[]{:S(2)}) %all-to-all-start.2) | async-done | bytes 524320 | tf_op jit(solution)/shard_map/all_to_all | solution.py:100
  130.5 1.7 reshape.349
  132.2 2.9 %fusion.6 = bf16[1,4,64,1,16,64]{5,1,4,2,3,0:T(4,128)(2,1)S(1)} fusion(bf16[64,16,4,4]{2,3,1,0:T(4,128)(2,1)} %copy-done.3, bf16[1,4,64,16,64]{4,3,2,1,0:T(8,128)(2,1)} %reshape.349), kind=kOutput, calls=%fused_computation.26 | convolution fusion | flops 2359296 | bytes 1081344 | tf_op jit(solution)/shard_map/transpose(jvp(cphfg,cgphd->cfphd))/dot_general | solution.py:42
  135.1 2.7 %fusion.4 = (f32[64,16,4]{2,1,0:T(8,128)S(1)}, bf16[64,16,4,4]{2,3,1,0:T(4,128)(2,1)S(1)}) fusion(f32[64,16,4,4]{2,3,1,0:T(4,128)S(1)} %get-tuple-element.15, f32[64,16,4]{2,1,0:T(8,128)S(1)} %copy-done.10, bf16[1,4,64,1,16,64]{5,4,3,2,1,0:T(8,128)(2,1)S(1)} %copy-done.9, bf16[1,4,64,16,64]{4,3,2,1,0:T(8,128)(2,1)S(1)} %copy-done.4), kind=kOutput, calls=%fused_computation.8 | convolution fusion | flops 2174976 | bytes 1179648 | tf_op jit(solution)/shard_map/transpose(jvp(cphfg,cgphd->cfphd))/dot_general | solution.py:42
  137.9 1.4 select_multiply_fusion
  139.3 1.2 fusion.7
  140.5 1.6 fusion.8
  142.2 3.1 %pad_add_fusion = bf16[1,4,64,3,16,64]{5,1,4,2,3,0:T(4,128)(2,1)S(1)} fusion(bf16[1,4,64,1,16,64]{5,1,4,2,3,0:T(4,128)(2,1)S(1)} %fusion.8, bf16[1,4,64,1,16,64]{5,1,4,2,3,0:T(4,128)(2,1)S(1)} %fusion.7, bf16[1,4,64,1,16,64]{5,1,4,2,3,0:T(4,128)(2,1)S(1)} %fusion.6), kind=kLoop, calls=%fused_computation.2 | loop fusion | flops 1572864 | bytes 3145728 | tf_op jit(solution)/shard_map/transpose(jvp())/add_any | solution.py:35
  145.7 3.2 %reshape.351 = bf16[256,3072]{1,0:T(8,128)(2,1)} reshape(bf16[1,4,64,3,16,64]{5,4,3,2,1,0:T(8,128)(2,1)S(1)} %copy.45) | data formatting | bytes 3145728 | tf_op jit(solution)/shard_map/transpose(jvp())/reshape;transpose(jvp())/reshape | solution.py:28
  149.0 5.9 %convolution_convert_fusion.6 = bf16[256,1024]{1,0:T(8,128)(2,1)} fusion(bf16[256,3072]{1,0:T(8,128)(2,1)} %reshape.351, bf16[1024,3072]{1,0:T(8,128)(2,1)} %all-gather.3.cloned.1.call-done), kind=kOutput, calls=%fused_computation.29 | convolution fusion | flops 1610874880 | bytes 8388608 | tf_op jit(solution)/shard_map/transpose(jvp())/dot_general | solution.py:27
  154.8 3.6 %all-to-all-start.3 = ((bf16[1,4,64,1024]{3,2,0,1:T(8,128)(2,1)}), bf16[1,4,64,1024]{3,2,0,1:T(8,128)(2,1)S(1)}, u32[]{:S(2)}, u32[]{:S(2)}) async-start(bf16[1,4,64,1024]{3,2,0,1:T(8,128)(2,1)} %bitcast.41), calls=%async_computation.3 | async-start | bytes 1048576 | tf_op jit(solution)/shard_map/all_to_all | solution.py:104
  158.6 0.7 pad_maximum_fusion
  159.5 12.7 %all-reduce.4 = (f32[8,32]{1,0:T(8,128)S(1)}, f32[8]{0:T(128)S(1)}) all-reduce(f32[8,32]{1,0:T(8,128)S(1)} %broadcast_multiply_fusion, f32[8]{0:T(128)S(1)} %compare_convert_fusion), channel_id=1, replica_groups=mesh['dp'=8,'tm'=4] {'tm'}, use_global_device_ids=true, to_apply=%region_8.9 | all-reduce | flops 264 | bytes 2112 | tf_op jit(solution)/shard_map/psum | solution.py:90
  172.2 12.3 %all-reduce.3 = (f32[8,32]{1,0:T(8,128)S(1)}, f32[8]{0:T(128)S(1)}) all-reduce(f32[8,32]{1,0:T(8,128)S(1)} %get-tuple-element.5, f32[8]{0:T(128)S(1)} %get-tuple-element.6), channel_id=1, replica_groups=mesh['dp'=8,'tm'=4] {'dp'}, use_global_device_ids=true, to_apply=%region_9.10 | all-reduce | flops 264 | bytes 2112 | tf_op jit(solution)/shard_map/psum | solution.py:89
  184.5 0.7 broadcast_divide_fusion
  185.2 13.3 %all-reduce.8.cloned.1.call-done = f32[2,1024,32]{1,2,0:T(8,128)} async-done(((f32[2,1024,32]{1,2,0:T(8,128)}), f32[2,1024,32]{1,2,0:T(8,128)}) %all-reduce.8.cloned.1.call-update) | async-done | bytes 262160 | tf_op jit(solution)/shard_map/psum | solution.py:90
  198.8 1.1 fusion.14
  200.0 55.3 %all-reduce.10.cloned.1.call-done = f32[2,1024,32]{1,2,0:T(8,128)} async-done(((f32[2,1024,32]{1,2,0:T(8,128)}), f32[2,1024,32]{1,2,0:T(8,128)}) %all-reduce.10.cloned.1.call-update) | async-done | bytes 262160 | tf_op jit(solution)/shard_map/psum | solution.py:89
  255.2 1.7 copy.87
  (49 shorter events, 4.1 us)
Async XLA Ops:
  7.2 79.9 %copy-start = (f32[8,32]{1,0:T(8,128)S(1)}, f32[8,32]{1,0:T(8,128)}, u32[]{:S(2)}) copy-start(f32[8,32]{1,0:T(8,128)} %param.12) | copy-start | bytes 3076
  7.2 50.8 %all-gather.3.cloned.1.call-start = ((), (), s32[]{:S(2)}) async-start(), calls=%async_computation.4 | async-start | bytes 7077888 | tf_op jit(solution)/shard_map/all_gather | solution.py:57
  17.5 20.8 %all-to-all-start = ((bf16[4,2,32768]{2,1,0:T(2,128)(2,1)}), bf16[4,2,32768]{2,1,0:T(2,128)(2,1)S(1)}, u32[]{:S(2)}, u32[]{:S(2)}) async-start(bf16[4,2,32768]{2,1,0:T(2,128)(2,1)} %reshape.366), calls=%async_computation | async-start | bytes 1048576 | tf_op jit(solution)/shard_map/all_to_all | solution.py:61
  23.9 63.8 %all-gather.5.cloned.1.call-start = ((), (), s32[]{:S(2)}) async-start(), calls=%async_computation.5 | async-start | bytes 2359296 | tf_op jit(solution)/shard_map/all_gather | solution.py:58
  74.8 1.6 copy-start.8
  75.4 1.0 copy-start.3
  78.0 23.4 %copy-start.1 = (bf16[1,1,256,1024]{3,2,1,0:T(8,128)(2,1)S(1)}, bf16[1,1,256,1024]{3,2,1,0:T(8,128)(2,1)}, u32[]{:S(2)}) copy-start(bf16[1,1,256,1024]{3,2,1,0:T(8,128)(2,1)} %param.7) | copy-start | bytes 1572868
  81.8 19.6 %all-to-all-start.1 = ((bf16[1,4,1,64,1024]{4,3,2,0,1:T(8,128)(2,1)}), bf16[1,4,1,64,1024]{4,3,2,0,1:T(8,128)(2,1)}, u32[]{:S(2)}, u32[]{:S(2)}) async-start(bf16[1,4,1,64,1024]{4,3,2,0,1:T(8,128)(2,1)} %bitcast.153), calls=%async_computation.1 | async-start | bytes 1048576 | tf_op jit(solution)/shard_map/all_to_all | solution.py:65
  86.4 19.0 %copy-start.5 = (f32[2,1024,32]{1,2,0:T(8,128)S(1)}, f32[2,1024,32]{1,2,0:T(8,128)}, u32[]{:S(2)}) copy-start(f32[2,1024,32]{1,2,0:T(8,128)} %param.11) | copy-start | bytes 786436
  101.4 11.7 %copy-start.11 = (bf16[1024,1024]{1,0:T(8,128)(2,1)S(1)}, bf16[1024,1024]{1,0:T(8,128)(2,1)}, u32[]{:S(2)}) copy-start(bf16[1024,1024]{1,0:T(8,128)(2,1)} %all-gather.5.cloned.1.call-done) | copy-start | bytes 6291460
  104.1 5.5 %collective-permute-start = (f32[1,1,1024]{2,1,0:T(1,128)S(1)}, f32[1,1,1024]{2,1,0:T(1,128)S(1)}, u32[]{:S(2)}, u32[]{:S(2)}) collective-permute-start(f32[1,1,1024]{2,1,0:T(1,128)S(1)} %bitcast.156), channel_id=1, source_target_pairs={{1,0},{2,1},{3,2},{5,4},{6,5},{7,6},{9,8},{10,9},{11,10},{13,12},{... | collective-permute-start | bytes 12296 | tf_op jit(solution)/shard_map/ppermute | solution.py:17
  110.0 3.0 %collective-permute-start.1 = (f32[1,1,1024]{2,1,0:T(1,128)S(1)}, f32[1,1,1024]{2,1,0:T(1,128)S(1)}, u32[]{:S(2)}, u32[]{:S(2)}) collective-permute-start(f32[1,1,1024]{2,1,0:T(1,128)S(1)} %convolution_bitcast_fusion.1), channel_id=1, source_target_pairs={{0,1},{1,2},{2,3},{4,5},{5,6},{6,7},{8,9},{9,10},{10,11},{12,13},{... | collective-permute-start | bytes 12296 | tf_op jit(solution)/shard_map/ppermute | solution.py:17
  114.7 15.8 %all-to-all-start.2 = ((bf16[1,1,4,64,1024]{4,3,1,0,2:T(8,128)(2,1)}), bf16[1,1,4,64,1024]{4,3,1,0,2:T(8,128)(2,1)S(1)}, u32[]{:S(2)}, u32[]{:S(2)}) async-start(bf16[1,1,4,64,1024]{4,3,1,0,2:T(8,128)(2,1)} %bitcast.155), calls=%async_computation.2 | async-start | bytes 1048576 | tf_op jit(solution)/shard_map/all_to_all | solution.py:100
  132.1 2.9 %copy-start.4 = (bf16[1,4,64,16,64]{4,3,2,1,0:T(8,128)(2,1)S(1)}, bf16[1,4,64,16,64]{4,3,2,1,0:T(8,128)(2,1)}, u32[]{:S(2)}) copy-start(bf16[1,4,64,16,64]{4,3,2,1,0:T(8,128)(2,1)} %reshape.349) | copy-start | bytes 1572868
  132.1 2.9 %copy-start.9 = (bf16[1,4,64,1,16,64]{5,4,3,2,1,0:T(8,128)(2,1)S(1)}, bf16[1,4,64,1,16,64]{5,4,3,2,1,0:T(8,128)(2,1)}, u32[]{:S(2)}) copy-start(bf16[1,4,64,1,16,64]{5,4,3,2,1,0:T(8,128)(2,1)} %get-tuple-element.7) | copy-start | bytes 1572868
  132.2 3.0 %copy-start.10 = (f32[64,16,4]{2,1,0:T(8,128)S(1)}, f32[64,16,4]{2,1,0:T(8,128)}, u32[]{:S(2)}) copy-start(f32[64,16,4]{2,1,0:T(8,128)} %multiply_divide_fusion) | copy-start | bytes 49156
  137.9 1.4 copy-start.7
  139.3 1.2 copy-start.6
  154.8 43.7 %copy-start.2 = (bf16[1,1,256,1024]{3,2,1,0:T(8,128)(2,1)S(1)}, bf16[1,1,256,1024]{3,2,1,0:T(8,128)(2,1)}, u32[]{:S(2)}) copy-start(bf16[1,1,256,1024]{3,2,1,0:T(8,128)(2,1)} %param.7) | copy-start | bytes 1572868
  154.8 43.7 %all-to-all-start.3 = ((bf16[1,4,64,1024]{3,2,0,1:T(8,128)(2,1)}), bf16[1,4,64,1024]{3,2,0,1:T(8,128)(2,1)S(1)}, u32[]{:S(2)}, u32[]{:S(2)}) async-start(bf16[1,4,64,1024]{3,2,0,1:T(8,128)(2,1)} %bitcast.41), calls=%async_computation.3 | async-start | bytes 1048576 | tf_op jit(solution)/shard_map/all_to_all | solution.py:104
  158.5 40.1 %all-reduce.8.cloned.1.call-start = ((), (), s32[]{:S(2)}) async-start(), calls=%async_computation.6 | async-start | bytes 524288 | tf_op jit(solution)/shard_map/psum | solution.py:90
  159.3 95.9 %all-reduce.10.cloned.1.call-start = ((), (), s32[]{:S(2)}) async-start(), calls=%async_computation.7 | async-start | bytes 524288 | tf_op jit(solution)/shard_map/psum | solution.py:89
Sparse Core Ops, SparseCore 0:
  9.9 48.1 all-gather.2
  59.9 27.7 all-gather.4
  162.2 36.3 all-reduce.7
  201.4 53.7 all-reduce.9
